TPU v7x, 256 devices: a whole 4x4x8 slice. The times are simulated.
256 devices in a mesh: grp: 64 (over y, x, z_lo, core), blk: 4 (over z_hi).
Axes of the slice: x: 4, y: 4, z: 8 (z_hi: 4, z_lo: 2; z = z_hi * 2 + z_lo), core: 2. Of those that a mesh axis runs over, the one named last changes fastest.
Arguments:
- tokens: bfloat16 [2048, 6144], P(('grp', 'blk')), may hold values from -6 to 6
- norm_gain: bfloat16 [6144], replicated, may hold values from 0.099609375 to 1.8984375
- expert_ids: int32 [2048, 2], P(('grp', 'blk')), may hold values from 0 to 7, all different within a row; in each aligned block of 8 rows (0 to 7, 8 to 15, ...) at most 3 rows name the same one
- combine: float32 [2048, 2], P(('grp', 'blk')), may hold values from 0.2 to 1
- w_gate: bfloat16 [6144, 65536], P(None, ('grp', 'blk')), may hold values from -0.078125 to 0.078125
- w_up: bfloat16 [6144, 65536], P(None, ('grp', 'blk')), may hold values from -0.078125 to 0.078125
- w_down: bfloat16 [65536, 6144], P(('grp', 'blk')), may hold values from -0.0625 to 0.0625
Outputs:
- layer_out: bfloat16 [2048, 6144], P(('grp', 'blk'))
Inputs may be any that keep to these rules, and one draw needn't show every extreme that they name: `expert_ids`: each row names 2 different experts; in the rows of one device no expert is named more than 3 times, a bound that some block reaches.
All inputs are finite; a program needn't handle non-finite values.
Results may differ from a plain program's by a relative error of at most 0.0075.
Values may be sent and summed in bfloat16 or wider, within the bound.
A program may use at most 128 MiB of HBM per device.

v0:
```python
import jax
import jax.numpy as jnp
from jax import lax
from jax.sharding import PartitionSpec as P

E = 8
TOP = 2
CAP = 3
epsilon = 1e-05


def in_order(blocks, dim):
    dims = list(blocks.shape[1:])
    dims[dim] *= blocks.shape[0]
    return jnp.moveaxis(blocks, 0, dim).reshape(dims)


def copy_for_each(x, axis):
    count = lax.axis_size(axis)
    return lax.all_to_all(jnp.broadcast_to(x[None], (count, *x.shape)), axis, 0, 0, tiled=True)


def gathered_copies(x, axis, dim):
    return in_order(copy_for_each(x, axis), dim)


def on_device(tokens, norm_gain, expert_ids, combine, w_gate, w_up, w_down):
    group_count = lax.axis_size("grp")
    per_group = group_count // E
    tok_count = tokens.shape[0]
    model_width = tokens.shape[1]
    wide_tokens = tokens.astype(jnp.float32)
    scale_rows = lax.rsqrt(jnp.mean(wide_tokens * wide_tokens, axis=1, keepdims=True) + epsilon)
    normed = (wide_tokens * scale_rows * norm_gain.astype(jnp.float32)[None, :]).astype(
        jnp.bfloat16
    )
    pair_rows = jnp.repeat(normed, TOP, axis=0)
    route_ids = expert_ids.reshape(tok_count * TOP)
    one_hot = (route_ids[:, None] == jnp.arange(E, dtype=jnp.int32)[None, :]).astype(jnp.int32)
    earlier = jnp.cumsum(one_hot, axis=0) - one_hot
    slot_index = jnp.sum(earlier * one_hot, axis=1)
    slot_match = (
        slot_index[None, None, :] == jnp.arange(CAP, dtype=jnp.int32)[None, :, None]
    ).astype(jnp.int32)
    placer = (one_hot.T[:, None, :] * slot_match).astype(jnp.bfloat16)
    buffer = jnp.einsum(
        "ecp,pd->ecd", placer, pair_rows, preferred_element_type=jnp.float32
    ).astype(jnp.bfloat16)
    stacked = gathered_copies(buffer[None], "blk", 0)
    outgoing = jnp.repeat(stacked, per_group, axis=1)
    arrived = lax.all_to_all(outgoing, "grp", split_axis=1, concat_axis=1, tiled=True)
    shard_rows = arrived.reshape(-1, model_width)
    gate_val = jnp.dot(shard_rows, w_gate, preferred_element_type=jnp.float32)
    up_val = jnp.dot(shard_rows, w_up, preferred_element_type=jnp.float32)
    hidden = (jax.nn.silu(gate_val) * up_val).astype(jnp.bfloat16)
    partial_value = jnp.dot(hidden, w_down, preferred_element_type=jnp.float32)
    rounded = lax.optimization_barrier(partial_value.astype(jnp.bfloat16))
    own_rows = lax.psum_scatter(
        rounded.astype(jnp.float32).astype(jnp.bfloat16), "blk", scatter_dimension=0, tiled=True
    ).astype(jnp.float32)
    home_terms = own_rows.reshape(group_count, CAP, model_width)
    returned = lax.all_to_all(
        home_terms.astype(jnp.bfloat16), "grp", split_axis=0, concat_axis=0, tiled=True
    ).astype(home_terms.dtype)
    expert_out = jnp.sum(returned.reshape(E, per_group, CAP, model_width), axis=1)
    pair_out = expert_out.reshape(E * CAP, model_width)[route_ids * CAP + slot_index]
    expert_mix = jnp.sum(
        pair_out.reshape(tok_count, TOP, model_width) * combine[:, :, None], axis=1
    )
    return (wide_tokens + expert_mix).astype(jnp.bfloat16)


def solution(mesh):
    return jax.shard_map(
        on_device,
        mesh=mesh,
        in_specs=(
            P(("grp", "blk"), None),
            P(),
            P(("grp", "blk"), None),
            P(("grp", "blk"), None),
            P(None, ("grp", "blk")),
            P(None, ("grp", "blk")),
            P(("grp", "blk"), None),
        ),
        out_specs=P(("grp", "blk"), None),
        check_vma=False,
    )
```

profile of v0, /device:TPU:1, one launch (start us, length us, event | category | flops | bytes accessed | tf_op | source)
XLA Modules:
  0.0 489.2 jit_solution(17626698553006937303)
XLA Ops:
  6.5 0.9 copy.16
  7.6 0.2 select_reduce_fusion
  7.8 0.7 convert_element_type.55
  8.5 1.1 fusion.1
  9.6 1.0 fusion.3
  10.8 0.2 convolution_convert_fusion.1
  11.1 36.6 %all_to_all.15 = bf16[4,1,8,3,6144]{4,2,3,1,0:T(8,128)(2,1)S(1)} all-to-all(bf16[4,1,8,3,6144]{4,2,3,1,0:T(8,128)(2,1)S(1)} %broadcast_in_dim.7), channel_id=1, replica_groups=mesh['grp'=64,'blk'=4] {'blk'}, dimensions={0} | all-to-all | bytes 2359296 | tf_op jit(solution)/shard_map/all_to_all | solution.py:20
  47.7 0.9 copy.17
  48.6 4.6 broadcast_in_dim.8
  53.3 119.6 %all_to_all.16 = bf16[4,64,3,6144]{3,0,2,1:T(4,128)(2,1)S(1)} all-to-all(bf16[4,64,3,6144]{3,0,2,1:T(4,128)(2,1)S(1)} %bitcast.26), channel_id=1, replica_groups=mesh['grp'=64,'blk'=4] {'grp'}, dimensions={1} | all-to-all | bytes 18874368 | tf_op jit(solution)/shard_map/all_to_all | solution.py:51
  172.8 25.3 %copy.18 = bf16[4,64,3,6144]{3,2,1,0:T(4,128)(2,1)} copy(bf16[4,64,3,6144]{3,0,2,1:T(4,128)(2,1)S(1)} %all_to_all.16) | data formatting | bytes 18874368 | tf_op jit(solution)/shard_map/all_to_all | solution.py:51
  198.2 23.5 %reshape.119 = bf16[768,6144]{1,0:T(8,128)(2,1)} reshape(bf16[4,64,3,6144]{3,2,1,0:T(4,128)(2,1)} %copy.18) | data formatting | bytes 18874368 | tf_op jit(solution)/shard_map/reshape | solution.py:52
  221.7 8.1 %fusion.11 = f32[768,256]{1,0:T(8,128)} fusion(bf16[768,6144]{1,0:T(8,128)(2,1)} %reshape.119, bf16[6144,256]{1,0:T(8,128)(2,1)} %param.11), kind=kOutput, calls=%fused_computation.30 | convolution fusion | flops 2415919104 | bytes 13369344 | tf_op jit(solution)/shard_map/dot_general | solution.py:53
  229.7 19.4 %convolution_convert_fusion = bf16[768,6144]{1,0:T(8,128)(2,1)} fusion(bf16[256,6144]{1,0:T(8,128)(2,1)S(1)} %copy-done, bf16[768,6144]{1,0:T(8,128)(2,1)} %reshape.119, bf16[6144,256]{1,0:T(8,128)(2,1)} %param.12, f32[768,256]{1,0:T(8,128)} %fusion.11), kind=kOutput, calls=%fused_computation.1 | convolution fusion | flops 4837736448 | bytes 25952256 | tf_op jit(solution)/shard_map/dot_general | solution.py:56
  249.1 163.2 %reduce-scatter.2.cloned.1.call-done = bf16[192,6144]{1,0:T(8,128)(2,1)} async-done(((bf16[768,6144]{1,0:T(8,128)(2,1)}), bf16[192,6144]{1,0:T(8,128)(2,1)}) %reduce-scatter.2.cloned.1.call-update) | async-done | bytes 2359312 | tf_op jit(solution)/shard_map/reduce_scatter | solution.py:58
  412.3 6.5 %convert_element_type.60 = bf16[64,3,6144]{2,1,0:T(4,128)(2,1)} reshape(bf16[192,6144]{1,0:T(8,128)(2,1)} %reduce-scatter.2.cloned.1.call-done) | data formatting | bytes 4718592 | tf_op jit(solution)/shard_map/convert_element_type | solution.py:63
  418.8 9.2 %all-to-all-start.2 = ((bf16[64,3,6144]{2,1,0:T(4,128)(2,1)}), bf16[64,3,6144]{2,1,0:T(4,128)(2,1)}, u32[]{:S(2)}, u32[]{:S(2)}) async-start(bf16[64,3,6144]{2,1,0:T(4,128)(2,1)} %convert_element_type.60), calls=%async_computation.3 | async-start | bytes 6291456 | tf_op jit(solution)/shard_map/all_to_all | solution.py:62
  428.3 41.3 %all-to-all-done.2 = bf16[64,3,6144]{2,1,0:T(4,128)(2,1)} async-done(((bf16[64,3,6144]{2,1,0:T(4,128)(2,1)}), bf16[64,3,6144]{2,1,0:T(4,128)(2,1)}, u32[]{:S(2)}, u32[]{:S(2)}) %all-to-all-start.2) | async-done | bytes 2359328 | tf_op jit(solution)/shard_map/all_to_all | solution.py:62
  469.6 4.5 convert_reduce_fusion
  474.1 2.2 reshape.122
  476.4 2.6 gather_fusion
  479.0 1.2 reshape.123
  480.2 0.6 multiply_reduce_fusion
  480.8 1.6 fusion.4
  (23 shorter events, 0.8 us)
Async XLA Ops:
  6.5 223.2 %copy-start = (bf16[256,6144]{1,0:T(8,128)(2,1)S(1)}, bf16[256,6144]{1,0:T(8,128)(2,1)}, u32[]{:S(2)}) copy-start(bf16[256,6144]{1,0:T(8,128)(2,1)} %param.13) | copy-start | bytes 9437188
  6.5 405.8 %reduce-scatter.2.cloned.1.call-start = ((), (), s32[]{:S(2)}) async-start(), calls=%async_computation.4 | async-start | bytes 11796480 | tf_op jit(solution)/shard_map/reduce_scatter | solution.py:58
  418.8 9.2 %copy-start.1 = (s32[8,2]{0,1:T(2,128)S(1)}, s32[8,2]{0,1:T(2,128)}, u32[]{:S(2)}) copy-start(s32[8,2]{0,1:T(2,128)} %param.9) | copy-start | bytes 196
  418.8 9.4 %copy-start.2 = (f32[8,2]{0,1:T(2,128)S(1)}, f32[8,2]{0,1:T(2,128)}, u32[]{:S(2)}) copy-start(f32[8,2]{0,1:T(2,128)} %param.10) | copy-start | bytes 196
  418.8 50.8 %all-to-all-start.2 = ((bf16[64,3,6144]{2,1,0:T(4,128)(2,1)}), bf16[64,3,6144]{2,1,0:T(4,128)(2,1)}, u32[]{:S(2)}, u32[]{:S(2)}) async-start(bf16[64,3,6144]{2,1,0:T(4,128)(2,1)} %convert_element_type.60), calls=%async_computation.3 | async-start | bytes 6291456 | tf_op jit(solution)/shard_map/all_to_all | solution.py:62
Sparse Core Ops, SparseCore 0:
  249.3 163.0 reduce-scatter.1
where the time goes:
time: 490 us; the launch traced here: 489 us
  waiting for transfers between devices  205 us (42%)
  blocking collectives  156 us (32%)
  local copies, waits for them, and re-layouts  68.5 us (14%)
  matrix products  27.6 us (6%)
  between operations  13.5 us (3%)
  other arithmetic  9.71 us (2%)
  starting transfers between devices  9.16 us (2%)
    reduce_scatter x1, waiting for transfers between devices, on_device(): lax.psum_scatter(rounded.astype(jnp.float32).astype(jnp.bfloat16), 'blk',...  163 us
    all_to_all x1, blocking collectives, on_device(): lax.all_to_all(outgoing, 'grp', split_axis=1, concat_axis=1, tiled=True)  120 us
    all_to_all x1, waiting for transfers between devices, on_device(): lax.all_to_all(home_terms.astype(jnp.bfloat16), 'grp', split_axis=0, conc...  41.3 us
    all_to_all x1, blocking collectives, copy_for_each(): lax.all_to_all(jnp.broadcast_to(x[None], (count, *x.shape)), axis, 0, 0,...  36.6 us
    all_to_all x1, local copies, waits for them, and re-layouts, on_device(): lax.all_to_all(outgoing, 'grp', split_axis=1, concat_axis=1, tiled=True)  25.3 us
    reshape x1, local copies, waits for them, and re-layouts, on_device(): shard_rows = arrived.reshape(-1, model_width)  23.5 us
    dot_general x1, matrix products, on_device(): partial_value = jnp.dot(hidden, w_down, preferred_element_type=jnp.float32)  19.4 us
  transfers between devices with their start and end apart: 2, of which 2 were waited for; matrix products, arithmetic and copies ran while one was open for 0% of the time, Pallas kernels for 0%

commit v1 on v0

--- a/solution.py
+++ b/solution.py
@@ -48,7 +48,19 @@
     ).astype(jnp.bfloat16)
     stacked = gathered_copies(buffer[None], "blk", 0)
     outgoing = jnp.repeat(stacked, per_group, axis=1)
-    arrived = lax.all_to_all(outgoing, "grp", split_axis=1, concat_axis=1, tiled=True)
+
+    def unite_row_here(row_dim, at_axis, m):
+        return jnp.concatenate(
+            lax.all_to_all(
+                jnp.stack(jnp.split(m, lax.axis_size("grp"), row_dim)),
+                axis_name="grp",
+                split_axis=0,
+                concat_axis=0,
+            ),
+            at_axis,
+        )
+
+    arrived = unite_row_here(1, 1, m=outgoing)
     shard_rows = arrived.reshape(-1, model_width)
     gate_val = jnp.dot(shard_rows, w_gate, preferred_element_type=jnp.float32)
     up_val = jnp.dot(shard_rows, w_up, preferred_element_type=jnp.float32)

time: 490 us -> 496 us (1.012)
    all_to_all x1 -> x0, local copies, waits for them, and re-layouts: 25.3 us -> none  [on_device(): lax.all_to_all(outgoing, 'grp', split_axis=1, concat_axis=1, tiled=True)]
    another operation x0 -> x2, local copies, waits for them, and re-layouts: none -> 23.6 us  [the longest x1 23.5 us: on_device(): shard_rows = arrived.reshape(-1, model_width)]
where the time goes in v1:
time: 496 us; the launch traced here: 494 us
  waiting for transfers between devices  205 us (41%)
  blocking collectives  156 us (31%)
  local copies, waits for them, and re-layouts  73 us (15%)
  matrix products  27.6 us (6%)
  between operations  13.6 us (3%)
  other arithmetic  9.71 us (2%)
  starting transfers between devices  9.23 us (2%)
    reduce_scatter x1, waiting for transfers between devices, on_device(): lax.psum_scatter(rounded.astype(jnp.float32).astype(jnp.bfloat16), 'blk',...  164 us
    all_to_all x1, blocking collectives, unite_row_here(): lax.all_to_all(jnp.stack(jnp.split(m, lax.axis_size('grp'), row_dim)), ax...  120 us
    all_to_all x1, waiting for transfers between devices, on_device(): lax.all_to_all(home_terms.astype(jnp.bfloat16), 'grp', split_axis=0, conc...  41.3 us
    all_to_all x1, blocking collectives, copy_for_each(): lax.all_to_all(jnp.broadcast_to(x[None], (count, *x.shape)), axis, 0, 0,...  36.6 us
    reshape x1, local copies, waits for them, and re-layouts, unite_row_here(): jnp.concatenate(lax.all_to_all(jnp.stack(jnp.split(m, lax.axis_size('grp'...  25.3 us
    another operation x1, local copies, waits for them, and re-layouts, on_device(): shard_rows = arrived.reshape(-1, model_width)  23.5 us
    dot_general x1, matrix products, on_device(): partial_value = jnp.dot(hidden, w_down, preferred_element_type=jnp.float32)  19.4 us
  transfers between devices with their start and end apart: 2, of which 2 were waited for; matrix products, arithmetic and copies ran while one was open for 0% of the time, Pallas kernels for 0%

profile of v1, /device:TPU:1, one launch (start us, length us, event | category | flops | bytes accessed | tf_op | source)
XLA Modules:
  0.0 494.5 jit_solution(17764920771073616513)
XLA Ops:
  6.5 0.9 copy.142
  7.6 0.2 select_reduce_fusion
  7.8 0.7 convert_element_type.55
  8.5 1.1 fusion.1
  9.6 1.0 fusion.3
  10.8 0.2 convolution_convert_fusion.1
  11.1 36.6 %all_to_all.15 = bf16[4,1,8,3,6144]{4,2,3,1,0:T(8,128)(2,1)S(1)} all-to-all(bf16[4,1,8,3,6144]{4,2,3,1,0:T(8,128)(2,1)S(1)} %broadcast_in_dim.7), channel_id=1, replica_groups=mesh['grp'=64,'blk'=4] {'blk'}, dimensions={0} | all-to-all | bytes 2359296 | tf_op jit(solution)/shard_map/all_to_all | solution.py:20
  47.7 0.9 copy.143
  48.6 4.6 broadcast_in_dim.8
  57.8 119.6 %all_to_all.16 = bf16[64,4,1,3,6144]{4,1,3,2,0:T(4,128)(2,1)S(1)} all-to-all(bf16[64,4,1,3,6144]{4,1,3,2,0:T(4,128)(2,1)S(1)} %fusion.5), channel_id=1, replica_groups=mesh['grp'=64,'blk'=4] {'grp'}, dimensions={0} | all-to-all | bytes 18874368 | tf_op jit(solution)/shard_map/all_to_all | solution.py:54
  177.4 25.3 %copy.144 = bf16[4,64,1,3,6144]{4,3,1,0,2:T(4,128)(2,1)} copy(bf16[4,64,1,3,6144]{4,0,3,2,1:T(4,128)(2,1)S(1)} %bitcast.285) | data formatting | bytes 18874368 | tf_op jit(solution)/shard_map/reshape | solution.py:53
  202.7 23.5 %reshape_reshape.3 = bf16[768,6144]{1,0:T(8,128)(2,1)} reshape(bf16[4,64,1,3,6144]{4,3,1,0,2:T(4,128)(2,1)} %copy.144) | data formatting | bytes 18874368 | tf_op jit(solution)/shard_map/reshape;reshape | solution.py:64
  226.2 8.1 %fusion.75 = f32[768,256]{1,0:T(8,128)} fusion(bf16[768,6144]{1,0:T(8,128)(2,1)} %reshape_reshape.3, bf16[6144,256]{1,0:T(8,128)(2,1)} %param.11), kind=kOutput, calls=%fused_computation.158 | convolution fusion | flops 2415919104 | bytes 13369344 | tf_op jit(solution)/shard_map/dot_general | solution.py:65
  234.3 19.4 %convolution_convert_fusion = bf16[768,6144]{1,0:T(8,128)(2,1)} fusion(bf16[256,6144]{1,0:T(8,128)(2,1)S(1)} %copy-done, bf16[768,6144]{1,0:T(8,128)(2,1)} %reshape_reshape.3, bf16[6144,256]{1,0:T(8,128)(2,1)} %param.12, f32[768,256]{1,0:T(8,128)} %fusion.75), kind=kOutput, calls=%fused_computation.1 | convolution fusion | flops 4837736448 | bytes 25952256 | tf_op jit(solution)/shard_map/dot_general | solution.py:68
  253.7 163.8 %reduce-scatter.2.cloned.1.call-done = bf16[192,6144]{1,0:T(8,128)(2,1)} async-done(((bf16[768,6144]{1,0:T(8,128)(2,1)}), bf16[192,6144]{1,0:T(8,128)(2,1)}) %reduce-scatter.2.cloned.1.call-update) | async-done | bytes 2359312 | tf_op jit(solution)/shard_map/reduce_scatter | solution.py:70
  417.6 6.5 %convert_element_type.60 = bf16[64,3,6144]{2,1,0:T(4,128)(2,1)} reshape(bf16[192,6144]{1,0:T(8,128)(2,1)} %reduce-scatter.2.cloned.1.call-done) | data formatting | bytes 4718592 | tf_op jit(solution)/shard_map/convert_element_type | solution.py:75
  424.0 9.2 %all-to-all-start.2 = ((bf16[64,3,6144]{2,1,0:T(4,128)(2,1)}), bf16[64,3,6144]{2,1,0:T(4,128)(2,1)}, u32[]{:S(2)}, u32[]{:S(2)}) async-start(bf16[64,3,6144]{2,1,0:T(4,128)(2,1)} %convert_element_type.60), calls=%async_computation.3 | async-start | bytes 6291456 | tf_op jit(solution)/shard_map/all_to_all | solution.py:74
  433.6 41.3 %all-to-all-done.2 = bf16[64,3,6144]{2,1,0:T(4,128)(2,1)} async-done(((bf16[64,3,6144]{2,1,0:T(4,128)(2,1)}), bf16[64,3,6144]{2,1,0:T(4,128)(2,1)}, u32[]{:S(2)}, u32[]{:S(2)}) %all-to-all-start.2) | async-done | bytes 2359328 | tf_op jit(solution)/shard_map/all_to_all | solution.py:74
  474.9 4.5 convert_reduce_fusion
  479.4 2.2 reshape.122
  481.6 2.6 gather_fusion
  484.3 1.2 reshape.123
  485.5 0.6 multiply_reduce_fusion
  486.1 1.6 fusion.4
  (87 shorter events, 5.3 us)
Async XLA Ops:
  6.5 227.8 %copy-start = (bf16[256,6144]{1,0:T(8,128)(2,1)S(1)}, bf16[256,6144]{1,0:T(8,128)(2,1)}, u32[]{:S(2)}) copy-start(bf16[256,6144]{1,0:T(8,128)(2,1)} %param.13) | copy-start | bytes 9437188
  6.5 411.0 %reduce-scatter.2.cloned.1.call-start = ((), (), s32[]{:S(2)}) async-start(), calls=%async_computation.4 | async-start | bytes 11796480 | tf_op jit(solution)/shard_map/reduce_scatter | solution.py:70
  253.7 179.6 %copy-start.1 = (s32[8,2]{0,1:T(2,128)S(1)}, s32[8,2]{0,1:T(2,128)}, u32[]{:S(2)}) copy-start(s32[8,2]{0,1:T(2,128)} %param.9) | copy-start | bytes 196
  253.7 179.8 %copy-start.2 = (f32[8,2]{0,1:T(2,128)S(1)}, f32[8,2]{0,1:T(2,128)}, u32[]{:S(2)}) copy-start(f32[8,2]{0,1:T(2,128)} %param.10) | copy-start | bytes 196
  424.0 50.8 %all-to-all-start.2 = ((bf16[64,3,6144]{2,1,0:T(4,128)(2,1)}), bf16[64,3,6144]{2,1,0:T(4,128)(2,1)}, u32[]{:S(2)}, u32[]{:S(2)}) async-start(bf16[64,3,6144]{2,1,0:T(4,128)(2,1)} %convert_element_type.60), calls=%async_computation.3 | async-start | bytes 6291456 | tf_op jit(solution)/shard_map/all_to_all | solution.py:74
Sparse Core Ops, SparseCore 0:
  253.8 163.6 reduce-scatter.1
